TPU v7x, 32 devices: a whole 2x2x4 slice. The times are simulated.
32 devices in a mesh: vrow: 8 (over z, y), vcol: 4 (over x, core).
Axes of the slice: x: 2, y: 2, z: 4, core: 2. Of those that a mesh axis runs over, the one named last changes fastest.
Arguments:
- policy_hidden: bfloat16 [1024, 3584], P(None, 'vcol'), may hold values from -400 to 400
- ref_hidden: bfloat16 [1024, 3584], P(None, 'vcol'), may hold values from -400 to 400
- mix_num: int32 [1024], replicated, may hold values from 0 to 16, as said below
- mix_den: int32 [1024], replicated, may hold values from 2 to 16
- policy_unembed: bfloat16 [3584, 16384], P(None, ('vrow', 'vcol')), may hold values from -0.09375 to 0.09375
- ref_unembed: bfloat16 [3584, 16384], P(None, ('vrow', 'vcol')), may hold values from -0.09375 to 0.09375
Outputs:
- mix_logprobs: float32 [1024, 16384], P(None, ('vrow', 'vcol'))
Inputs may be any that keep to these rules, and one draw needn't show every extreme that they name: Each sequence's mix_num is at most its mix_den.
All inputs are finite; a program needn't handle non-finite values.
Results may differ from a plain program's by a relative error of at most 0.0003.
Values may be sent and summed in bfloat16 or wider, within the bound.
No kernel may reach another device: no remote copies, remote signals or barrier semaphores. Data moves between devices by JAX's collectives and lax.ppermute only.
A program may use at most 64 MiB of HBM per device.

v0:
```python
import jax
import jax.numpy as jnp
from jax import lax
from jax.sharding import PartitionSpec as P


def merged(value, axis, join):
    pieces = jax.tree.map(lambda part: lax.all_gather(part, axis), value)
    head = jax.tree.map(lambda part: part[0], pieces)
    tail = jax.tree.map(lambda part: part[1:], pieces)
    running, _ = lax.scan(lambda running, slab: (join(running, slab), None), head, tail)
    return running


def combine_stats(first, second):
    high = jnp.maximum(first[0], second[0])
    total = first[1] * jnp.exp(first[0] - high) + second[1] * jnp.exp(second[0] - high)
    return (high, total)


def body(policy_hidden, ref_hidden, mix_num, mix_den, policy_unembed, ref_unembed):
    policy_full, ref_full = (
        lax.all_gather(policy_hidden, "vcol", axis=1, tiled=True),
        lax.all_gather(ref_hidden, "vcol", axis=1, tiled=True),
    )
    policy_logits = jnp.dot(policy_full, policy_unembed, preferred_element_type=jnp.float32)
    ref_logits = jnp.dot(ref_full, ref_unembed, preferred_element_type=jnp.float32)
    beta = (mix_num.astype(jnp.float32) / mix_den.astype(jnp.float32))[:, None]
    mixed = (1.0 - beta) * policy_logits + beta * ref_logits
    local_top = jnp.max(mixed, axis=1, keepdims=True)
    local_total = jnp.sum(jnp.exp(mixed - local_top), axis=1, keepdims=True)
    top, total = merged((local_top, local_total), ("vrow", "vcol"), combine_stats)
    return mixed - top - jnp.log(total)


def solution(mesh):
    return jax.shard_map(
        body,
        mesh=mesh,
        in_specs=(
            P(None, "vcol"),
            P(None, "vcol"),
            P(),
            P(),
            P(None, ("vrow", "vcol")),
            P(None, ("vrow", "vcol")),
        ),
        out_specs=P(None, ("vrow", "vcol")),
        check_vma=False,
    )
```

profile of v0, /device:TPU:0, one launch (start us, length us, event | category | flops | bytes accessed | tf_op | source)
XLA Modules:
  0.0 217.9 jit_solution(10455677230840361698)
XLA Ops:
  6.5 0.0 copy-start.1
  6.5 0.0 copy-start
  6.5 0.0 all-gather.5.cloned.1.call-start
  6.5 0.7 all-gather.5.cloned.1.call-update
  7.3 0.0 all-gather.7.cloned.1.call-start
  7.3 0.7 all-gather.7.cloned.1.call-update
  8.0 0.0 copy-done.1
  8.0 0.0 copy-done
  8.0 55.9 %all-gather.5.cloned.1.call-done = bf16[1024,3584]{1,0:T(8,128)(2,1)} async-done(((bf16[1024,896]{1,0:T(8,128)(2,1)}), bf16[1024,3584]{1,0:T(8,128)(2,1)}) %all-gather.5.cloned.1.call-update) | async-done | bytes 7340048 | tf_op jit(solution)/shard_map/all_gather | solution.py:23
  63.9 9.4 %fusion.3 = f32[1024,512]{0,1:T(8,128)} fusion(bf16[1024,3584]{1,0:T(8,128)(2,1)} %all-gather.5.cloned.1.call-done, bf16[3584,512]{1,0:T(8,128)(2,1)} %param.12), kind=kOutput, calls=%fused_computation.11 | convolution fusion | flops 3758096384 | bytes 13107200 | tf_op jit(solution)/shard_map/dot_general | solution.py:26
  73.4 44.4 %all-gather.7.cloned.1.call-done = bf16[1024,3584]{1,0:T(8,128)(2,1)} async-done(((bf16[1024,896]{1,0:T(8,128)(2,1)}), bf16[1024,3584]{1,0:T(8,128)(2,1)}) %all-gather.7.cloned.1.call-update) | async-done | bytes 7340048 | tf_op jit(solution)/shard_map/all_gather | solution.py:24
  117.8 8.8 %fusion.2 = (f32[1024]{0:T(1024)S(1)}, f32[1024,512]{0,1:T(8,128)S(1)}) fusion(bf16[1024,3584]{1,0:T(8,128)(2,1)} %all-gather.7.cloned.1.call-done, bf16[3584,512]{1,0:T(8,128)(2,1)} %param.13, f32[1024]{0:T(1024)S(1)} %get-tuple-element.48, f32[1024,512]{0,1:T(8,128)} %fusion.3, f32[1024]{0:T(1024)S(1)} %get-tuple-element.47), kind=kOutput, calls=%fused_computation.10 | convolution fusion | flops 3760192512 | bytes 15216640 | tf_op jit(solution)/shard_map/dot_general | solution.py:27
  126.6 0.3 exponential_reduce_fusion
  126.9 40.9 %all-gather.1 = f32[32768]{0:T(1024)S(1)} all-gather(f32[1024]{0:T(1024)S(1)} %exponential_reduce_fusion), channel_id=3, replica_groups=mesh['vrow'=8,'vcol'=4] {'vrow','vcol'}, dimensions={0}, use_global_device_ids=true | all-gather | bytes 135168 | tf_op jit(solution)/shard_map/all_gather | solution.py:8
  167.8 37.0 %all-gather = f32[32768]{0:T(1024)S(1)} all-gather(f32[1024]{0:T(1024)S(1)} %get-tuple-element.49), channel_id=2, replica_groups=mesh['vrow'=8,'vcol'=4] {'vrow','vcol'}, dimensions={0}, use_global_device_ids=true | all-gather | bytes 135168 | tf_op jit(solution)/shard_map/all_gather | solution.py:8
  204.9 1.6 while.12
  206.5 1.6 subtract_subtract_fusion
  208.1 2.9 %copy.8 = f32[1024,512]{1,0:T(8,128)} copy(f32[1024,512]{0,1:T(8,128)} %subtract_subtract_fusion) | data formatting | bytes 4194304 | tf_op jit(solution)/shard_map/sub | solution.py:33
  (37 shorter events, 1.2 us)
Async XLA Ops:
  6.5 1.5 copy-start.1
  6.5 1.5 copy-start
  6.5 57.4 %all-gather.5.cloned.1.call-start = ((), (), s32[]{:S(2)}) async-start(), calls=%async_computation | async-start | bytes 9175040 | tf_op jit(solution)/shard_map/all_gather | solution.py:23
  7.3 110.5 %all-gather.7.cloned.1.call-start = ((), (), s32[]{:S(2)}) async-start(), calls=%async_computation.1 | async-start | bytes 9175040 | tf_op jit(solution)/shard_map/all_gather | solution.py:24
Sparse Core Ops, SparseCore 0:
  8.9 54.9 all-gather.4
  65.5 52.2 all-gather.6
where the time goes:
time: 218 us
  waiting for transfers between devices  102 us (47%)
  blocking collectives  77.9 us (36%)
  matrix products  18.3 us (8%)
  between operations  13.5 us (6%)
  other arithmetic  3.1 us (1%)
  local copies, waits for them, and re-layouts  2.92 us (1%)
    all_gather x2, blocking collectives, merged(): pieces = jax.tree.map(lambda part: lax.all_gather(part, axis), value)  77.9 us
    all_gather x1, waiting for transfers between devices, body(): lax.all_gather(policy_hidden, 'vcol', axis=1, tiled=True)  55.9 us
    all_gather x1, waiting for transfers between devices, body(): lax.all_gather(ref_hidden, 'vcol', axis=1, tiled=True)  44.4 us
    dot_general x1, matrix products, body(): jnp.dot(policy_full, policy_unembed, preferred_element_type=jnp.float32)  9.43 us
    dot_general x1, matrix products, body(): jnp.dot(ref_full, ref_unembed, preferred_element_type=jnp.float32)  8.83 us
  transfers between devices with their start and end apart: 2, of which 2 were waited for; matrix products, arithmetic and copies ran while one was open for 4% of the time, Pallas kernels for 0%

commit v1 on v0

v1 whole, which is shorter than its diff:
```python
import jax
import jax.numpy as jnp
from jax import lax
from jax.sharding import PartitionSpec as P

AXES = ("vrow", "vcol")
PART1 = 96


def dotf(a, b):
    return jnp.dot(a, b, preferred_element_type=jnp.float32)


def make_body(rows_of, cols_of):
    chips = cols_of // 2

    def route(move):
        return [
            (r * cols_of + c, (lambda t: t[0] * cols_of + t[1])(move(r, c)))
            for r in range(rows_of)
            for c in range(cols_of)
        ]

    over_core = route(lambda r, c: (r, c ^ 1))
    over_y = route(lambda r, c: (r ^ 1, c))
    over_z = route(lambda r, c: (r ^ 2, c))

    def over_x(step):
        return route(lambda r, c: (r, (c - 2 * step) % cols_of))

    def send(value, pairs):
        return lax.ppermute(value, AXES, pairs)

    def body(policy_hidden, ref_hidden, mix_num, mix_den, policy_unembed, ref_unembed):
        batch, feats = policy_hidden.shape
        vocab = policy_unembed.shape[1]
        hidden = (policy_hidden, ref_hidden)
        unembed = (policy_unembed, ref_unembed)
        quarter = batch // 4
        first = quarter * PART1 // 256
        second = quarter - first
        col = lax.axis_index("vcol")
        core = col % 2
        chip = col // 2
        me = lax.axis_index("vrow") % 4
        beta = (mix_num.astype(jnp.float32) / mix_den.astype(jnp.float32))[:, None]

        def rows(value, j, lo, n):
            return lax.dynamic_slice_in_dim(value, (me ^ j) * quarter + lo, n, 0)

        def columns(weight, shard):
            return lax.dynamic_slice_in_dim(weight, shard * feats, feats, 0)

        steps = range(1, chips)
        x1 = {d: [send(rows(h, 0, 0, first), over_x(d)) for h in hidden] for d in steps}
        x2 = {d: [send(rows(h, 0, first, second), over_x(d)) for h in hidden] for d in steps}
        xd = {d: [send(rows(h, 3, first, second), over_x(d)) for h in hidden] for d in steps}

        shards = [((chip + d) % chips) * 2 for d in range(chips)]
        other = [[send(columns(w, s + 1 - core), over_core) for w in unembed] for s in shards]
        own = [[columns(w, s + core) for w in unembed] for s in shards]

        y1 = {d: [send(v, over_y) for v in x1[d]] for d in steps}
        z1 = {d: [send(v, over_z) for v in x1[d]] for d in steps}
        d1 = {d: [send(z1[d][0], over_y), send(y1[d][1], over_z)] for d in steps}
        y2 = {d: [send(v, over_y) for v in x2[d]] for d in steps}
        z2 = {d: [send(v, over_z) for v in x2[d]] for d in steps}

        def mix(b, policy, ref):
            return (1.0 - b) * policy + b * ref

        def local(weights):
            return mix(beta, dotf(hidden[0], weights[0]), dotf(hidden[1], weights[1]))

        near = (local(own[0]), local(other[0]))
        early = [(0, 0, first, x1), (0, first, second, x2), (1, 0, first, y1), (2, 0, first, z1), (3, 0, first, d1), (3, first, second, xd)]
        late = [(1, first, second, y2), (2, first, second, z2)]

        def logits(pieces):
            pick = lambda value: jnp.concatenate([rows(value, j, lo, n) for j, lo, n, _ in pieces], axis=0)
            b = pick(beta)
            out = []
            for side, weights in ((0, own), (1, other)):
                total = pick(near[side])
                for d in steps:
                    got = [jnp.concatenate([p[3][d][m] for p in pieces], axis=0) for m in range(2)]
                    total = total + mix(b, dotf(got[0], weights[d][0]), dotf(got[1], weights[d][1]))
                out.append(total)
            return out[0] + send(out[1], over_core)

        groups = [(early, logits(early)), (late, logits(late))]
        block = {}
        for pieces, value in groups:
            at = 0
            for j, lo, n, _ in pieces:
                block[j, lo] = value[at : at + n]
                at += n
        by_offset = jnp.stack([jnp.concatenate([block[j, 0], block[j, first]], axis=0) for j in range(4)])
        mixed = jnp.concatenate([lax.dynamic_index_in_dim(by_offset, me ^ q, 0, keepdims=False) for q in range(4)], axis=0)

        top = jnp.max(mixed, axis=1)
        total = jnp.sum(jnp.exp(mixed - top[:, None]), axis=1)
        part = top + jnp.log(total)
        n_dev = rows_of * cols_of
        spread = jnp.broadcast_to(part.reshape(1, 8, batch // 8), (n_dev, 8, batch // 8))
        parts = lax.all_to_all(spread, AXES, 0, 0).reshape(n_dev, batch)
        high = jnp.max(parts, axis=0)
        lse = high + jnp.log(jnp.sum(jnp.exp(parts - high), axis=0))
        return mixed - lse[:, None]

    return body


def solution(mesh):
    return jax.shard_map(
        make_body(mesh.shape["vrow"], mesh.shape["vcol"]),
        mesh=mesh,
        in_specs=(
            P(None, "vcol"),
            P(None, "vcol"),
            P(),
            P(),
            P(None, ("vrow", "vcol")),
            P(None, ("vrow", "vcol")),
        ),
        out_specs=P(None, ("vrow", "vcol")),
        check_vma=False,
    )
```

time: 218 us -> 102 us (0.47)
  waiting for transfers between devices: 102 us -> 24.2 us
  blocking collectives: 77.9 us -> 12.1 us
  starting transfers between devices: 0.04 us -> 21.9 us
  local copies, waits for them, and re-layouts: 2.92 us -> 19.3 us
  between operations: 13.5 us -> 0.58 us
    all_gather x2 -> x0, waiting for transfers between devices: 100 us -> none  [the longest x1 55.9 us: body(): lax.all_gather(policy_hidden, 'vcol', axis=1, tiled=True)]
    all_gather x2 -> x0, blocking collectives: 77.9 us -> none  [merged(): pieces = jax.tree.map(lambda part: lax.all_gather(part, axis), value)]
    ppermute x0 -> x22, waiting for transfers between devices: none -> 24.2 us  [send(): return lax.ppermute(value, AXES, pairs)]
    ppermute x0 -> x22, starting transfers between devices: none -> 21.9 us  [send(): return lax.ppermute(value, AXES, pairs)]
    all_to_all x0 -> x1, blocking collectives: none -> 12.1 us  [body(): parts = lax.all_to_all(spread, AXES, 0, 0).reshape(n_dev, batch)]
    dynamic_slice x0 -> x8, local copies, waits for them, and re-layouts: none -> 10.3 us  [the longest x6 6.02 us: rows(): return lax.dynamic_slice_in_dim(value, (me ^ j) * quarter + lo, n, 0)]
    unnamed x4 -> x58, local copies, waits for them, and re-layouts: 0.01 us -> 5.59 us
    concatenate x0 -> x10, local copies, waits for them, and re-layouts: none -> 2.99 us  [the longest x6 2.87 us: logits(): jnp.concatenate([rows(value, j, lo, n) for j, lo, n, _ in pieces], axis=0)]
  transfers between devices with their start and end apart: 2 -> 22, of which waited for: 2 -> 9; matrix products, arithmetic and copies ran while one was open for 4% -> 32% of each run, Pallas kernels for 0% -> 0%
where the time goes in v1:
time: 102 us; the launch traced here: 101 us
  waiting for transfers between devices  24.2 us (24%)
  starting transfers between devices  21.9 us (21%)
  local copies, waits for them, and re-layouts  19.3 us (19%)
  matrix products  18.2 us (18%)
  blocking collectives  12.1 us (12%)
  other arithmetic  4.83 us (5%)
    ppermute x22, waiting for transfers between devices, send(): return lax.ppermute(value, AXES, pairs)  24.2 us
    ppermute x22, starting transfers between devices, send(): return lax.ppermute(value, AXES, pairs)  21.9 us
    dot_general x12, matrix products, dotf(): return jnp.dot(a, b, preferred_element_type=jnp.float32)  18.2 us
    all_to_all x1, blocking collectives, body(): parts = lax.all_to_all(spread, AXES, 0, 0).reshape(n_dev, batch)  12.1 us
    dynamic_slice x6, local copies, waits for them, and re-layouts, rows(): return lax.dynamic_slice_in_dim(value, (me ^ j) * quarter + lo, n, 0)  6.02 us
    unnamed x58, local copies, waits for them, and re-layouts  5.59 us
    dynamic_slice x2, local copies, waits for them, and re-layouts, columns(): return lax.dynamic_slice_in_dim(weight, shard * feats, feats, 0)  4.33 us
    concatenate x6, local copies, waits for them, and re-layouts, logits(): jnp.concatenate([rows(value, j, lo, n) for j, lo, n, _ in pieces], axis=0)  2.87 us
  transfers between devices with their start and end apart: 22, of which 9 were waited for; matrix products, arithmetic and copies ran while one was open for 32% of the time, Pallas kernels for 0%

profile of v1, /device:TPU:0, one launch (start us, length us, event | category | flops | bytes accessed | tf_op | source)
XLA Modules:
  0.0 101.0 jit_solution(1282801030879699551)
XLA Ops:
  0.0 3.0 %constant_dynamic-slice_fusion.1 = (bf16[896,512]{1,0:T(8,128)(2,1)}, bf16[896,512]{1,0:T(8,128)(2,1)}) fusion(bf16[3584,512]{1,0:T(8,128)(2,1)} %param.10, s32[]{:T(128)S(6)} %select_n.112, s32[]{:T(128)S(6)} %select_n.111), kind=kLoop, calls=%fused_computation.76 | loop fusion | bytes 3670024 | tf_op jit(solution)/shard_map/dynamic_slice | solution.py:52
  3.5 1.4 %constant_dynamic-slice_fusion = (bf16[896,512]{1,0:T(8,128)(2,1)}, bf16[896,512]{1,0:T(8,128)(2,1)}) fusion(bf16[3584,512]{1,0:T(8,128)(2,1)S(1)} %copy-done.1, s32[]{:T(128)S(6)} %select_n.112, s32[]{:T(128)S(6)} %select_n.111), kind=kLoop, calls=%fused_computation.75 | loop fusion | bytes 3670024 | tf_op jit(solution)/shard_map/dynamic_slice | solution.py:52
  4.9 1.9 %constant_dynamic-slice_fusion.4 = (bf16[160,896]{1,0:T(8,128)(2,1)}, bf16[160,896]{1,0:T(8,128)(2,1)}) fusion(bf16[1024,896]{1,0:T(8,128)(2,1)} %param.7, s32[]{:T(128)S(6)} %select_n.108, s32[]{:T(128)S(6)} %select_n.104), kind=kLoop, calls=%fused_computation.80 | loop fusion | bytes 1146888 | tf_op jit(solution)/shard_map/dynamic_slice | solution.py:49
  6.8 3.0 %collective-permute-start.7 = (bf16[160,896]{1,0:T(8,128)(2,1)}, bf16[160,896]{1,0:T(8,128)(2,1)}, u32[]{:S(2)}, u32[]{:S(2)}) collective-permute-start(bf16[160,896]{1,0:T(8,128)(2,1)} %get-tuple-element.22), channel_id=1, source_target_pairs={{0,2},{1,3},{2,0},{3,1},{4,6},{5,7},{6,4},{7,5},{8,10},{9,11},{10,... | collective-permute-start | bytes 860168 | tf_op jit(solution)/shard_map/ppermute | solution.py:32
  9.7 1.6 %constant_dynamic-slice_fusion.6 = bf16[96,896]{1,0:T(8,128)(2,1)} fusion(bf16[1024,896]{1,0:T(8,128)(2,1)} %param.7, s32[]{:T(128)S(6)} %select_n.103), kind=kLoop, calls=%fused_computation.82 | loop fusion | bytes 344068 | tf_op jit(solution)/shard_map/dynamic_slice | solution.py:49
  12.1 2.0 %collective-permute-start = (bf16[96,896]{1,0:T(8,128)(2,1)}, bf16[96,896]{1,0:T(8,128)(2,1)}, u32[]{:S(2)}, u32[]{:S(2)}) collective-permute-start(bf16[96,896]{1,0:T(8,128)(2,1)} %constant_dynamic-slice_fusion.9), channel_id=1, source_target_pairs={{0,2},{1,3},{2,0},{3,1},{4,6},{5,7},{6,4},{7,5},{8,10},{9,11},{10,... | collective-permute-start | bytes 516104 | tf_op jit(solution)/shard_map/ppermute | solution.py:32
  14.9 3.8 %fusion.10 = f32[512,1024]{0,1:T(8,128)} fusion(bf16[1024,896]{1,0:T(8,128)(2,1)S(1)} %copy-done.7, bf16[3584,512]{1,0:T(8,128)(2,1)} %param.10, s32[]{:T(128)S(6)} %select_n.101), kind=kOutput, calls=%fused_computation.24 | convolution fusion | flops 939524096 | bytes 4849668 | tf_op jit(solution)/shard_map/dot_general | solution.py:11
  19.4 3.7 %multiply_add_fusion.1 = f32[512,1024]{0,1:T(8,128)S(1)} fusion(f32[512,1024]{0,1:T(8,128)} %fusion.10, bf16[1024,896]{1,0:T(8,128)(2,1)} %param.7, f32[1024]{0:T(1024)S(1)} %get-tuple-element.6, f32[1024]{0:T(1024)S(1)} %get-tuple-element.5, bf16[3584,512]{1,0:T(8,128)(2,1)} %param.11, s32[]{:T(128)S(6)} %select_n.101), kind=kOutput, calls=%fused_computation.4 | convolution fusion | flops 941096960 | bytes 6955012 | tf_op jit(solution)/shard_map/dot_general | solution.py:11
  28.5 0.9 constant_dynamic-update-slice_fusion.11
  29.4 2.1 %collective-permute-start.11 = (bf16[160,896]{1,0:T(8,128)(2,1)}, bf16[160,896]{1,0:T(8,128)(2,1)S(1)}, u32[]{:S(2)}, u32[]{:S(2)}) collective-permute-start(bf16[160,896]{1,0:T(8,128)(2,1)} %get-tuple-element.21), channel_id=1, source_target_pairs={{0,2},{1,3},{2,0},{3,1},{4,6},{5,7},{6,4},{7,5},{8,10},{9,11},{10,... | collective-permute-start | bytes 860168 | tf_op jit(solution)/shard_map/ppermute | solution.py:32
  32.4 1.6 %collective-permute-start.8 = (bf16[96,896]{1,0:T(8,128)(2,1)}, bf16[96,896]{1,0:T(8,128)(2,1)S(1)}, u32[]{:S(2)}, u32[]{:S(2)}) collective-permute-start(bf16[96,896]{1,0:T(8,128)(2,1)} %collective-permute-done.6), channel_id=1, source_target_pairs={{0,4},{1,5},{2,6},{3,7},{4,0},{5,1},{6,2},{7,3},{8,12},{9,13},{10,... | collective-permute-start | bytes 516104 | tf_op jit(solution)/shard_map/ppermute | solution.py:32
  34.0 1.0 constant_dynamic-update-slice_fusion.10
  35.0 3.3 %collective-permute-done.1 = bf16[160,896]{1,0:T(8,128)(2,1)S(1)} collective-permute-done((bf16[160,896]{1,0:T(8,128)(2,1)}, bf16[160,896]{1,0:T(8,128)(2,1)S(1)}, u32[]{:S(2)}, u32[]{:S(2)}) %collective-permute-start.1) | collective-permute-done | bytes 286752 | tf_op jit(solution)/shard_map/ppermute | solution.py:32
  38.4 1.6 %collective-permute-start.9 = (bf16[96,896]{1,0:T(8,128)(2,1)}, bf16[96,896]{1,0:T(8,128)(2,1)S(1)}, u32[]{:S(2)}, u32[]{:S(2)}) collective-permute-start(bf16[96,896]{1,0:T(8,128)(2,1)} %collective-permute-done.6), channel_id=1, source_target_pairs={{0,8},{1,9},{2,10},{3,11},{4,12},{5,13},{6,14},{7,15},{8,0},{9,1},... | collective-permute-start | bytes 516104 | tf_op jit(solution)/shard_map/ppermute | solution.py:32
  40.0 1.6 %collective-permute-start.2 = (bf16[96,896]{1,0:T(8,128)(2,1)}, bf16[96,896]{1,0:T(8,128)(2,1)S(1)}, u32[]{:S(2)}, u32[]{:S(2)}) collective-permute-start(bf16[96,896]{1,0:T(8,128)(2,1)} %collective-permute-done), channel_id=1, source_target_pairs={{0,4},{1,5},{2,6},{3,7},{4,0},{5,1},{6,2},{7,3},{8,12},{9,13},{10,... | collective-permute-start | bytes 516104 | tf_op jit(solution)/shard_map/ppermute | solution.py:32
  41.6 3.9 %collective-permute-done.9 = bf16[96,896]{1,0:T(8,128)(2,1)S(1)} collective-permute-done((bf16[96,896]{1,0:T(8,128)(2,1)}, bf16[96,896]{1,0:T(8,128)(2,1)S(1)}, u32[]{:S(2)}, u32[]{:S(2)}) %collective-permute-start.9) | collective-permute-done | bytes 172064 | tf_op jit(solution)/shard_map/ppermute | solution.py:32
  45.5 1.6 %collective-permute-start.3 = (bf16[96,896]{1,0:T(8,128)(2,1)}, bf16[96,896]{1,0:T(8,128)(2,1)S(1)}, u32[]{:S(2)}, u32[]{:S(2)}) collective-permute-start(bf16[96,896]{1,0:T(8,128)(2,1)} %collective-permute-done), channel_id=1, source_target_pairs={{0,8},{1,9},{2,10},{3,11},{4,12},{5,13},{6,14},{7,15},{8,0},{9,1},... | collective-permute-start | bytes 516104 | tf_op jit(solution)/shard_map/ppermute | solution.py:32
  47.7 3.5 %collective-permute-done.3 = bf16[96,896]{1,0:T(8,128)(2,1)S(1)} collective-permute-done((bf16[96,896]{1,0:T(8,128)(2,1)}, bf16[96,896]{1,0:T(8,128)(2,1)S(1)}, u32[]{:S(2)}, u32[]{:S(2)}) %collective-permute-start.3) | collective-permute-done | bytes 172064 | tf_op jit(solution)/shard_map/ppermute | solution.py:32
  51.3 1.7 %collective-permute-done.10 = bf16[96,896]{1,0:T(8,128)(2,1)S(1)} collective-permute-done((bf16[96,896]{1,0:T(8,128)(2,1)S(1)}, bf16[96,896]{1,0:T(8,128)(2,1)S(1)}, u32[]{:S(2)}, u32[]{:S(2)}) %collective-permute-start.10) | collective-permute-done | bytes 172064 | tf_op jit(solution)/shard_map/ppermute | solution.py:32
  53.0 1.6 %collective-permute-start.4 = (bf16[96,896]{1,0:T(8,128)(2,1)S(1)}, bf16[96,896]{1,0:T(8,128)(2,1)S(1)}, u32[]{:S(2)}, u32[]{:S(2)}) collective-permute-start(bf16[96,896]{1,0:T(8,128)(2,1)S(1)} %collective-permute-done.3), channel_id=1, source_target_pairs={{0,4},{1,5},{2,6},{3,7},{4,0},{5,1},{6,2},{7,3},{8,12},{9,13},{10,... | collective-permute-start | bytes 516104 | tf_op jit(solution)/shard_map/ppermute | solution.py:32
  55.1 4.8 %collective-permute-done.4 = bf16[96,896]{1,0:T(8,128)(2,1)S(1)} collective-permute-done((bf16[96,896]{1,0:T(8,128)(2,1)S(1)}, bf16[96,896]{1,0:T(8,128)(2,1)S(1)}, u32[]{:S(2)}, u32[]{:S(2)}) %collective-permute-start.4) | collective-permute-done | bytes 172064 | tf_op jit(solution)/shard_map/ppermute | solution.py:32
  59.9 1.5 %collective-permute-start.17 = (bf16[160,896]{1,0:T(8,128)(2,1)S(1)}, bf16[160,896]{1,0:T(8,128)(2,1)S(1)}, u32[]{:S(2)}, u32[]{:S(2)}) collective-permute-start(bf16[160,896]{1,0:T(8,128)(2,1)S(1)} %collective-permute-done.1), channel_id=1, source_target_pairs={{0,4},{1,5},{2,6},{3,7},{4,0},{5,1},{6,2},{7,3},{8,12},{9,13},{10,... | collective-permute-start | bytes 860168 | tf_op jit(solution)/shard_map/ppermute | solution.py:32
  61.5 1.6 %collective-permute-start.20 = (bf16[160,896]{1,0:T(8,128)(2,1)}, bf16[160,896]{1,0:T(8,128)(2,1)S(1)}, u32[]{:S(2)}, u32[]{:S(2)}) collective-permute-start(bf16[160,896]{1,0:T(8,128)(2,1)} %collective-permute-done.7), channel_id=1, source_target_pairs={{0,8},{1,9},{2,10},{3,11},{4,12},{5,13},{6,14},{7,15},{8,0},{9,1},... | collective-permute-start | bytes 860168 | tf_op jit(solution)/shard_map/ppermute | solution.py:32
  63.2 1.4 %collective-permute-start.18 = (bf16[160,896]{1,0:T(8,128)(2,1)S(1)}, bf16[160,896]{1,0:T(8,128)(2,1)S(1)}, u32[]{:S(2)}, u32[]{:S(2)}) collective-permute-start(bf16[160,896]{1,0:T(8,128)(2,1)S(1)} %collective-permute-done.1), channel_id=1, source_target_pairs={{0,8},{1,9},{2,10},{3,11},{4,12},{5,13},{6,14},{7,15},{8,0},{9,1},... | collective-permute-start | bytes 860168 | tf_op jit(solution)/shard_map/ppermute | solution.py:32
  64.6 2.0 %collective-permute-done.17 = bf16[160,896]{1,0:T(8,128)(2,1)S(1)} collective-permute-done((bf16[160,896]{1,0:T(8,128)(2,1)S(1)}, bf16[160,896]{1,0:T(8,128)(2,1)S(1)}, u32[]{:S(2)}, u32[]{:S(2)}) %collective-permute-start.17) | collective-permute-done | bytes 286752 | tf_op jit(solution)/shard_map/ppermute | solution.py:32
  66.6 1.8 %collective-permute-done.20 = bf16[160,896]{1,0:T(8,128)(2,1)S(1)} collective-permute-done((bf16[160,896]{1,0:T(8,128)(2,1)}, bf16[160,896]{1,0:T(8,128)(2,1)S(1)}, u32[]{:S(2)}, u32[]{:S(2)}) %collective-permute-start.20) | collective-permute-done | bytes 286752 | tf_op jit(solution)/shard_map/ppermute | solution.py:32
  68.5 3.0 %collective-permute-done.18 = bf16[160,896]{1,0:T(8,128)(2,1)S(1)} collective-permute-done((bf16[160,896]{1,0:T(8,128)(2,1)S(1)}, bf16[160,896]{1,0:T(8,128)(2,1)S(1)}, u32[]{:S(2)}, u32[]{:S(2)}) %collective-permute-start.18) | collective-permute-done | bytes 286752 | tf_op jit(solution)/shard_map/ppermute | solution.py:32
  71.6 2.5 %fusion.27 = f32[512,1024]{0,1:T(8,128)S(1)} fusion(bf16[1024,896]{1,0:T(8,128)(2,1)S(1)} %copy-done.8, bf16[896,512]{1,0:T(8,128)(2,1)} %collective-permute-done.12), kind=kOutput, calls=%fused_computation.100 | convolution fusion | flops 939524096 | bytes 4849664 | tf_op jit(solution)/shard_map/dot_general | solution.py:11
  74.1 2.4 %multiply_add_fusion = f32[512,1024]{0,1:T(8,128)S(1)} fusion(f32[512,1024]{0,1:T(8,128)S(1)} %fusion.27, bf16[1024,896]{1,0:T(8,128)(2,1)S(1)} %copy-done.9, bf16[896,512]{1,0:T(8,128)(2,1)} %collective-permute-done.13, f32[1024]{0:T(1024)S(1)} %get-tuple-element.6, f32[1024]{0:T(1024)S(1)} %copy-done.17), kind=kOutput, calls=%fused_computation.3 | convolution fusion | flops 941096960 | bytes 6955008 | tf_op jit(solution)/shard_map/dot_general | solution.py:11
  84.8 1.0 %fusion.4 = f32[704,512]{1,0:T(8,128)S(1)} fusion(f32[704,512]{1,0:T(8,128)S(1)} %collective-permute-done.16, f32[704,512]{1,0:T(8,128)S(1)} %bitcast_dynamic-update-slice_fusion.2, f32[704,512]{1,0:T(8,128)S(1)} %convolution_multiply_fusion.2, bf16[704,896]{1,0:T(8,128)(2,1)S(1)} %constant_dynamic-update-slice_fusion, bf16[3584,512]{1,0:T(8,128)(2,1)S(1)} %copy-done, ...), kind=kOutput, calls=%fused_computation.13 | convolution fusion | flops 647364608 | bytes 7950340 | tf_op jit(solution)/shard_map/dot_general | solution.py:11
  87.4 12.1 %all_to_all.5 = f32[32,8,128]{2,1,0:T(8,128)S(1)} all-to-all(f32[32,8,128]{2,1,0:T(8,128)S(1)} %broadcast_in_dim.2), channel_id=1, replica_groups=mesh['vrow'=8,'vcol'=4] {'vrow','vcol'}, dimensions={0} | all-to-all | bytes 262144 | tf_op jit(solution)/shard_map/all_to_all | solution.py:106
  99.5 1.5 %broadcast_subtract_fusion = f32[1024,512]{1,0:T(8,128)} fusion(f32[1024]{0:T(1024)S(1)} %add_bitcast_fusion, f32[256,512]{1,0:T(8,128)S(1)} %get-tuple-element.12, f32[256,512]{1,0:T(8,128)S(1)} %get-tuple-element.13, f32[256,512]{1,0:T(8,128)S(1)} %get-tuple-element.14, f32[256,512]{1,0:T(8,128)S(1)} %get-tuple-element.11), kind=kLoop, calls=%fused_computation.22 | loop fusion | flops 2097152 | bytes 4198400 | tf_op jit(solution)/shard_map/sub | solution.py:109
  (120 shorter events, 20.1 us)
Async XLA Ops:
  3.0 68.6 %collective-permute-start.12 = (bf16[896,512]{1,0:T(8,128)(2,1)}, bf16[896,512]{1,0:T(8,128)(2,1)}, u32[]{:S(2)}, u32[]{:S(2)}) collective-permute-start(bf16[896,512]{1,0:T(8,128)(2,1)} %get-tuple-element.8), channel_id=1, source_target_pairs={{0,1},{1,0},{2,3},{3,2},{4,5},{5,4},{6,7},{7,6},{8,9},{9,8},{10,11... | collective-permute-start | bytes 2752520 | tf_op jit(solution)/shard_map/ppermute | solution.py:32
  3.5 7.9 %copy-start.7 = (bf16[1024,896]{1,0:T(8,128)(2,1)S(1)}, bf16[1024,896]{1,0:T(8,128)(2,1)}, u32[]{:S(2)}) copy-start(bf16[1024,896]{1,0:T(8,128)(2,1)} %param.6) | copy-start | bytes 5505028
  4.8 69.3 %collective-permute-start.13 = (bf16[896,512]{1,0:T(8,128)(2,1)}, bf16[896,512]{1,0:T(8,128)(2,1)}, u32[]{:S(2)}, u32[]{:S(2)}) collective-permute-start(bf16[896,512]{1,0:T(8,128)(2,1)} %get-tuple-element.10), channel_id=1, source_target_pairs={{0,1},{1,0},{2,3},{3,2},{4,5},{5,4},{6,7},{7,6},{8,9},{9,8},{10,11... | collective-permute-start | bytes 2752520 | tf_op jit(solution)/shard_map/ppermute | solution.py:32
  6.8 25.7 %collective-permute-start.7 = (bf16[160,896]{1,0:T(8,128)(2,1)}, bf16[160,896]{1,0:T(8,128)(2,1)}, u32[]{:S(2)}, u32[]{:S(2)}) collective-permute-start(bf16[160,896]{1,0:T(8,128)(2,1)} %get-tuple-element.22), channel_id=1, source_target_pairs={{0,2},{1,3},{2,0},{3,1},{4,6},{5,7},{6,4},{7,5},{8,10},{9,11},{10,... | collective-permute-start | bytes 860168 | tf_op jit(solution)/shard_map/ppermute | solution.py:32
  11.4 17.0 %collective-permute-start.6 = (bf16[96,896]{1,0:T(8,128)(2,1)}, bf16[96,896]{1,0:T(8,128)(2,1)}, u32[]{:S(2)}, u32[]{:S(2)}) collective-permute-start(bf16[96,896]{1,0:T(8,128)(2,1)} %constant_dynamic-slice_fusion.6), channel_id=1, source_target_pairs={{0,2},{1,3},{2,0},{3,1},{4,6},{5,7},{6,4},{7,5},{8,10},{9,11},{10,... | collective-permute-start | bytes 516104 | tf_op jit(solution)/shard_map/ppermute | solution.py:32
  12.1 17.4 %collective-permute-start = (bf16[96,896]{1,0:T(8,128)(2,1)}, bf16[96,896]{1,0:T(8,128)(2,1)}, u32[]{:S(2)}, u32[]{:S(2)}) collective-permute-start(bf16[96,896]{1,0:T(8,128)(2,1)} %constant_dynamic-slice_fusion.9), channel_id=1, source_target_pairs={{0,2},{1,3},{2,0},{3,1},{4,6},{5,7},{6,4},{7,5},{8,10},{9,11},{10,... | collective-permute-start | bytes 516104 | tf_op jit(solution)/shard_map/ppermute | solution.py:32
  14.9 3.8 %copy-start.14 = (s32[1024]{0:T(1024)S(1)}, s32[1024]{0:T(1024)}, u32[]{:S(2)}) copy-start(s32[1024]{0:T(1024)} %param.9) | copy-start | bytes 12292
  14.9 3.8 %copy-start.15 = (s32[1024]{0:T(1024)S(1)}, s32[1024]{0:T(1024)}, u32[]{:S(2)}) copy-start(s32[1024]{0:T(1024)} %param.8) | copy-start | bytes 12292
  18.7 4.3 %copy-start.16 = (f32[1024]{0:T(1024)}, f32[1024]{0:T(1024)S(1)}, u32[]{:S(2)}) copy-start(f32[1024]{0:T(1024)S(1)} %get-tuple-element.5) | copy-start | bytes 12292
  19.4 5.3 %copy-start.12 = (f32[160]{0:T(256)}, f32[160]{0:T(256)S(1)}, u32[]{:S(2)}) copy-start(f32[160]{0:T(256)S(1)} %get-tuple-element.31) | copy-start | bytes 1924
  19.4 6.2 %copy-start.11 = (f32[160]{0:T(256)}, f32[160]{0:T(256)S(1)}, u32[]{:S(2)}) copy-start(f32[160]{0:T(256)S(1)} %get-tuple-element.29) | copy-start | bytes 1924
  27.6 23.5 %copy-start.10 = (bf16[160,896]{1,0:T(8,128)(2,1)S(1)}, bf16[160,896]{1,0:T(8,128)(2,1)}, u32[]{:S(2)}) copy-start(bf16[160,896]{1,0:T(8,128)(2,1)} %get-tuple-element.19) | copy-start | bytes 860164
  28.4 10.0 %collective-permute-start.1 = (bf16[160,896]{1,0:T(8,128)(2,1)}, bf16[160,896]{1,0:T(8,128)(2,1)S(1)}, u32[]{:S(2)}, u32[]{:S(2)}) collective-permute-start(bf16[160,896]{1,0:T(8,128)(2,1)} %get-tuple-element.20), channel_id=1, source_target_pairs={{0,2},{1,3},{2,0},{3,1},{4,6},{5,7},{6,4},{7,5},{8,10},{9,11},{10,... | collective-permute-start | bytes 860168 | tf_op jit(solution)/shard_map/ppermute | solution.py:32
  29.4 25.1 %collective-permute-start.11 = (bf16[160,896]{1,0:T(8,128)(2,1)}, bf16[160,896]{1,0:T(8,128)(2,1)S(1)}, u32[]{:S(2)}, u32[]{:S(2)}) collective-permute-start(bf16[160,896]{1,0:T(8,128)(2,1)} %get-tuple-element.21), channel_id=1, source_target_pairs={{0,2},{1,3},{2,0},{3,1},{4,6},{5,7},{6,4},{7,5},{8,10},{9,11},{10,... | collective-permute-start | bytes 860168 | tf_op jit(solution)/shard_map/ppermute | solution.py:32
  32.4 7.5 %collective-permute-start.8 = (bf16[96,896]{1,0:T(8,128)(2,1)}, bf16[96,896]{1,0:T(8,128)(2,1)S(1)}, u32[]{:S(2)}, u32[]{:S(2)}) collective-permute-start(bf16[96,896]{1,0:T(8,128)(2,1)} %collective-permute-done.6), channel_id=1, source_target_pairs={{0,4},{1,5},{2,6},{3,7},{4,0},{5,1},{6,2},{7,3},{8,12},{9,13},{10,... | collective-permute-start | bytes 516104 | tf_op jit(solution)/shard_map/ppermute | solution.py:32
  38.4 7.1 %collective-permute-start.9 = (bf16[96,896]{1,0:T(8,128)(2,1)}, bf16[96,896]{1,0:T(8,128)(2,1)S(1)}, u32[]{:S(2)}, u32[]{:S(2)}) collective-permute-start(bf16[96,896]{1,0:T(8,128)(2,1)} %collective-permute-done.6), channel_id=1, source_target_pairs={{0,8},{1,9},{2,10},{3,11},{4,12},{5,13},{6,14},{7,15},{8,0},{9,1},... | collective-permute-start | bytes 516104 | tf_op jit(solution)/shard_map/ppermute | solution.py:32
  40.0 7.1 %collective-permute-start.2 = (bf16[96,896]{1,0:T(8,128)(2,1)}, bf16[96,896]{1,0:T(8,128)(2,1)S(1)}, u32[]{:S(2)}, u32[]{:S(2)}) collective-permute-start(bf16[96,896]{1,0:T(8,128)(2,1)} %collective-permute-done), channel_id=1, source_target_pairs={{0,4},{1,5},{2,6},{3,7},{4,0},{5,1},{6,2},{7,3},{8,12},{9,13},{10,... | collective-permute-start | bytes 516104 | tf_op jit(solution)/shard_map/ppermute | solution.py:32
  45.5 5.6 %collective-permute-start.3 = (bf16[96,896]{1,0:T(8,128)(2,1)}, bf16[96,896]{1,0:T(8,128)(2,1)S(1)}, u32[]{:S(2)}, u32[]{:S(2)}) collective-permute-start(bf16[96,896]{1,0:T(8,128)(2,1)} %collective-permute-done), channel_id=1, source_target_pairs={{0,8},{1,9},{2,10},{3,11},{4,12},{5,13},{6,14},{7,15},{8,0},{9,1},... | collective-permute-start | bytes 516104 | tf_op jit(solution)/shard_map/ppermute | solution.py:32
  47.1 5.8 %collective-permute-start.10 = (bf16[96,896]{1,0:T(8,128)(2,1)S(1)}, bf16[96,896]{1,0:T(8,128)(2,1)S(1)}, u32[]{:S(2)}, u32[]{:S(2)}) collective-permute-start(bf16[96,896]{1,0:T(8,128)(2,1)S(1)} %collective-permute-done.8), channel_id=1, source_target_pairs={{0,8},{1,9},{2,10},{3,11},{4,12},{5,13},{6,14},{7,15},{8,0},{9,1},... | collective-permute-start | bytes 516104 | tf_op jit(solution)/shard_map/ppermute | solution.py:32
  47.7 18.9 %copy-start.6 = (bf16[896,512]{1,0:T(8,128)(2,1)S(1)}, bf16[896,512]{1,0:T(8,128)(2,1)}, u32[]{:S(2)}) copy-start(bf16[896,512]{1,0:T(8,128)(2,1)} %get-tuple-element.9) | copy-start | bytes 2752516
  51.1 10.4 %collective-permute-start.5 = (bf16[160,896]{1,0:T(8,128)(2,1)S(1)}, bf16[160,896]{1,0:T(8,128)(2,1)S(1)}, u32[]{:S(2)}, u32[]{:S(2)}) collective-permute-start(bf16[160,896]{1,0:T(8,128)(2,1)S(1)} %copy-done.10), channel_id=1, source_target_pairs={{0,2},{1,3},{2,0},{3,1},{4,6},{5,7},{6,4},{7,5},{8,10},{9,11},{10,... | collective-permute-start | bytes 860168 | tf_op jit(solution)/shard_map/ppermute | solution.py:32
  51.2 17.2 %copy-start.5 = (bf16[896,512]{1,0:T(8,128)(2,1)S(1)}, bf16[896,512]{1,0:T(8,128)(2,1)}, u32[]{:S(2)}) copy-start(bf16[896,512]{1,0:T(8,128)(2,1)} %get-tuple-element.7) | copy-start | bytes 2752516
  53.0 7.0 %collective-permute-start.4 = (bf16[96,896]{1,0:T(8,128)(2,1)S(1)}, bf16[96,896]{1,0:T(8,128)(2,1)S(1)}, u32[]{:S(2)}, u32[]{:S(2)}) collective-permute-start(bf16[96,896]{1,0:T(8,128)(2,1)S(1)} %collective-permute-done.3), channel_id=1, source_target_pairs={{0,4},{1,5},{2,6},{3,7},{4,0},{5,1},{6,2},{7,3},{8,12},{9,13},{10,... | collective-permute-start | bytes 516104 | tf_op jit(solution)/shard_map/ppermute | solution.py:32
  54.6 8.6 %collective-permute-start.19 = (bf16[160,896]{1,0:T(8,128)(2,1)}, bf16[160,896]{1,0:T(8,128)(2,1)S(1)}, u32[]{:S(2)}, u32[]{:S(2)}) collective-permute-start(bf16[160,896]{1,0:T(8,128)(2,1)} %collective-permute-done.7), channel_id=1, source_target_pairs={{0,4},{1,5},{2,6},{3,7},{4,0},{5,1},{6,2},{7,3},{8,12},{9,13},{10,... | collective-permute-start | bytes 860168 | tf_op jit(solution)/shard_map/ppermute | solution.py:32
  59.9 6.6 %collective-permute-start.17 = (bf16[160,896]{1,0:T(8,128)(2,1)S(1)}, bf16[160,896]{1,0:T(8,128)(2,1)S(1)}, u32[]{:S(2)}, u32[]{:S(2)}) collective-permute-start(bf16[160,896]{1,0:T(8,128)(2,1)S(1)} %collective-permute-done.1), channel_id=1, source_target_pairs={{0,4},{1,5},{2,6},{3,7},{4,0},{5,1},{6,2},{7,3},{8,12},{9,13},{10,... | collective-permute-start | bytes 860168 | tf_op jit(solution)/shard_map/ppermute | solution.py:32
  61.5 10.1 %copy-start.8 = (bf16[1024,896]{1,0:T(8,128)(2,1)S(1)}, bf16[1024,896]{1,0:T(8,128)(2,1)}, u32[]{:S(2)}) copy-start(bf16[1024,896]{1,0:T(8,128)(2,1)} %param.6) | copy-start | bytes 5505028
  61.5 6.9 %collective-permute-start.20 = (bf16[160,896]{1,0:T(8,128)(2,1)}, bf16[160,896]{1,0:T(8,128)(2,1)S(1)}, u32[]{:S(2)}, u32[]{:S(2)}) collective-permute-start(bf16[160,896]{1,0:T(8,128)(2,1)} %collective-permute-done.7), channel_id=1, source_target_pairs={{0,8},{1,9},{2,10},{3,11},{4,12},{5,13},{6,14},{7,15},{8,0},{9,1},... | collective-permute-start | bytes 860168 | tf_op jit(solution)/shard_map/ppermute | solution.py:32
  63.2 8.3 %collective-permute-start.18 = (bf16[160,896]{1,0:T(8,128)(2,1)S(1)}, bf16[160,896]{1,0:T(8,128)(2,1)S(1)}, u32[]{:S(2)}, u32[]{:S(2)}) collective-permute-start(bf16[160,896]{1,0:T(8,128)(2,1)S(1)} %collective-permute-done.1), channel_id=1, source_target_pairs={{0,8},{1,9},{2,10},{3,11},{4,12},{5,13},{6,14},{7,15},{8,0},{9,1},... | collective-permute-start | bytes 860168 | tf_op jit(solution)/shard_map/ppermute | solution.py:32
  66.6 10.3 %collective-permute-start.15 = (bf16[896,512]{1,0:T(8,128)(2,1)S(1)}, bf16[896,512]{1,0:T(8,128)(2,1)S(1)}, u32[]{:S(2)}, u32[]{:S(2)}) collective-permute-start(bf16[896,512]{1,0:T(8,128)(2,1)S(1)} %copy-done.6), channel_id=1, source_target_pairs={{0,1},{1,0},{2,3},{3,2},{4,5},{5,4},{6,7},{7,6},{8,9},{9,8},{10,11... | collective-permute-start | bytes 2752520 | tf_op jit(solution)/shard_map/ppermute | solution.py:32
  68.4 9.9 %collective-permute-start.14 = (bf16[896,512]{1,0:T(8,128)(2,1)S(1)}, bf16[896,512]{1,0:T(8,128)(2,1)S(1)}, u32[]{:S(2)}, u32[]{:S(2)}) collective-permute-start(bf16[896,512]{1,0:T(8,128)(2,1)S(1)} %copy-done.5), channel_id=1, source_target_pairs={{0,1},{1,0},{2,3},{3,2},{4,5},{5,4},{6,7},{7,6},{8,9},{9,8},{10,11... | collective-permute-start | bytes 2752520 | tf_op jit(solution)/shard_map/ppermute | solution.py:32
  79.2 5.6 %collective-permute-start.16 = (f32[704,512]{1,0:T(8,128)S(1)}, f32[704,512]{1,0:T(8,128)S(1)}, u32[]{:S(2)}, u32[]{:S(2)}) collective-permute-start(f32[704,512]{1,0:T(8,128)S(1)} %fusion.1), channel_id=1, source_target_pairs={{0,1},{1,0},{2,3},{3,2},{4,5},{5,4},{6,7},{7,6},{8,9},{9,8},{10,11... | collective-permute-start | bytes 4325384 | tf_op jit(solution)/shard_map/ppermute | solution.py:32
  80.3 3.1 %collective-permute-start.21 = (f32[320,512]{1,0:T(8,128)S(1)}, f32[320,512]{1,0:T(8,128)S(1)}, u32[]{:S(2)}, u32[]{:S(2)}) collective-permute-start(f32[320,512]{1,0:T(8,128)S(1)} %maximum_add_fusion), channel_id=1, source_target_pairs={{0,1},{1,0},{2,3},{3,2},{4,5},{5,4},{6,7},{7,6},{8,9},{9,8},{10,11... | collective-permute-start | bytes 1966088 | tf_op jit(solution)/shard_map/ppermute | solution.py:32
  (8 other events, 16.3 us)
